TPU v7x, 128 devices: a whole 4x4x4 slice. The times are simulated.
128 devices in a mesh: vocab: 32 (over z, x, core), tok: 4 (over y).
Axes of the slice: x: 4, y: 4, z: 4, core: 2. Of those that a mesh axis runs over, the one named last changes fastest.
Arguments:
- hidden: bfloat16 [512, 8192], P('tok'), may hold values from -40 to 40
- head: bfloat16 [8192, 126976], P('tok', 'vocab'), may hold values from -0.06629126 to 0.06629126
- teacher_probs: bfloat16 [512, 151552], P('tok', 'vocab'), may hold values from 0.0009994507 to 1
- tile_values: bfloat16 [1536, 128, 128], P('vocab'), may hold values from 0.049804688 to 1
- tile_list: int32 [1536, 2], replicated, may hold values from 0 to 991, as said below
- token_ids: int32 [512], P('tok'), may hold values from 0 to 126975
Outputs:
- token_loss: float32 [512], P('tok')
- hidden_grad: float32 [512, 8192], P('vocab', 'tok')
Inputs may be any that keep to these rules, and one draw needn't show every extreme that they name: `tile_list`: column 0 is a row tile in 0 to 36, column 1 a student column tile. Of the 48 tiles of one source, at most 4 have column tiles owned by one vocab index (index c // 31), and every source gives exactly 4 to each of 8 indices.
All inputs are finite; a program needn't handle non-finite values.
Results may differ from a plain program's by a relative error of at most 0.00056.
Values may be sent and summed in bfloat16 or wider, within the bound.
A program may use at most 128 MiB of HBM per device.

v0:
```python
import jax
import jax.numpy as jnp
from jax import lax
from jax.sharding import PartitionSpec as P

TILE = 128
CAP = 4


hard_weight = 0.5
loss_scale = 64.0


def sent_to_all(shard, axis):
    count = lax.axis_size(axis)
    return lax.all_to_all(
        jnp.broadcast_to(shard[None], (count, *shard.shape)), axis, 0, 0, tiled=True
    )


def gathered_once(shard, axis):
    leaves = jax.tree.leaves(shard)
    sequence = sorted(range(len(leaves)), key=lambda k: -leaves[k].size)
    width = (1, *leaves[sequence[0]].shape)[-1]
    lines = [
        jnp.pad(leaves[k].reshape(-1), (0, -leaves[k].size % width)).reshape(-1, width)
        for k in sequence
    ]
    both, at, found = (sent_to_all(jnp.concatenate(lines), axis), 0, {})
    for k, line in zip(sequence, lines):
        slab = both[:, at : at + len(line)].reshape(len(both), -1)
        found[k] = slab[:, : leaves[k].size].reshape(-1, *leaves[k].shape)
        at += len(line)
    numbers = iter(range(len(leaves)))
    return jax.tree.map(lambda _: found[next(numbers)], shard)


def joined_by_halves(pieces, combine):
    while len(jax.tree.leaves(pieces)[0]) > 1:
        pieces = jax.vmap(combine)(
            *(jax.tree.map(lambda part: part[side::2], pieces) for side in (0, 1))
        )
    return jax.tree.map(lambda part: part[0], pieces)


def combined_all(shard, axis, combine):
    pieces = gathered_once(shard, axis)
    return joined_by_halves(pieces, combine)


def combine_stats(left_side, right_side):
    top_left, total_left = (left_side[0], left_side[1])
    top_right, total_right = (right_side[0], right_side[1])
    row_top = jnp.maximum(top_left, top_right)
    exp_total = total_left * jnp.exp(top_left - row_top) + total_right * jnp.exp(
        top_right - row_top
    )
    return (row_top, exp_total) + tuple((a + b for a, b in zip(left_side[2:], right_side[2:])))


def on_device(hidden, head, teacher_probs, tile_values, tile_list, token_ids):
    tok_count = hidden.shape[0]
    vocab_part = head.shape[1]
    n_vocab = lax.axis_size("vocab")
    me_vocab = lax.axis_index("vocab")
    capacity = CAP
    blocks_dev = vocab_part // TILE
    tiles_here = tile_values.shape[0]
    features = lax.all_to_all(hidden, "tok", split_axis=1, concat_axis=0, tiled=True)
    rows = features
    logits = lax.psum_scatter(
        jnp.dot(rows, head, preferred_element_type=jnp.float32),
        "tok",
        scatter_dimension=0,
        tiled=True,
    )
    all_pairs = tile_list.reshape(n_vocab, tiles_here, 2)
    all_owner = all_pairs[:, :, 1] // blocks_dev
    matches = all_owner[:, :, None] == all_owner[:, None, :]
    positions = jnp.arange(tiles_here, dtype=jnp.int32)
    earlier_mask = positions[None, :] < positions[:, None]
    earlier = jnp.sum(jnp.where(matches & earlier_mask[None], 1, 0), axis=2).astype(jnp.int32)
    slot_index = all_owner * capacity + earlier
    my_slots = lax.dynamic_index_in_dim(slot_index, me_vocab, 0, keepdims=False)
    my_pairs = lax.dynamic_index_in_dim(all_pairs, me_vocab, 0, keepdims=False)
    teacher_blocks = teacher_probs.reshape(tok_count, teacher_probs.shape[1] // TILE, TILE)
    row_select = (
        my_pairs[:, 0][:, None] == jnp.arange(teacher_blocks.shape[1], dtype=jnp.int32)[None, :]
    )
    row_select = row_select.astype(jnp.bfloat16)
    chosen = jnp.einsum(
        "st,ktc->skc", row_select, teacher_blocks, preferred_element_type=jnp.float32
    )
    chosen = chosen.astype(jnp.bfloat16)
    products = jnp.einsum("skc,scd->skd", chosen, tile_values, preferred_element_type=jnp.float32)
    products = products.astype(jnp.bfloat16)
    send_select = jnp.arange(n_vocab * capacity, dtype=jnp.int32)[:, None] == my_slots[None, :]
    send_select = send_select.astype(jnp.bfloat16)
    outgoing = jnp.einsum("rs,skd->rkd", send_select, products, preferred_element_type=jnp.float32)
    outgoing = outgoing.astype(jnp.bfloat16)
    received = lax.all_to_all(outgoing, "vocab", split_axis=0, concat_axis=0, tiled=True)
    sources = jnp.arange(n_vocab, dtype=jnp.int32)[:, None]
    is_valid = all_owner == me_vocab
    recv_key = jnp.where(is_valid, sources * capacity + earlier, -1).reshape(-1)
    local_col = (all_pairs[:, :, 1] - me_vocab * blocks_dev).reshape(-1)
    key_table = recv_key[:, None] == jnp.arange(n_vocab * capacity, dtype=jnp.int32)[None, :]
    col_table = local_col[:, None] == jnp.arange(blocks_dev, dtype=jnp.int32)[None, :]
    selector = jnp.einsum("ar,aj->rj", key_table.astype(jnp.float32), col_table.astype(jnp.float32))
    selector = selector.astype(jnp.bfloat16)
    mapped = jnp.einsum("rkc,rj->kjc", received, selector, preferred_element_type=jnp.float32)
    mapped = mapped.reshape(tok_count, vocab_part)
    columns = jnp.arange(vocab_part, dtype=jnp.int32)[None, :] + me_vocab * vocab_part
    is_target = columns == token_ids[:, None]
    positive = mapped > 0
    mass = jnp.sum(mapped, axis=1)
    self_term = jnp.sum(
        jnp.where(positive, mapped * jnp.log(jnp.where(positive, mapped, 1.0)), 0.0), axis=1
    )
    cross_term = jnp.sum(mapped * logits, axis=1)
    target = jnp.sum(jnp.where(is_target, logits, 0.0), axis=1)
    local_top = jnp.max(logits, axis=1)
    local_total = jnp.sum(jnp.exp(logits - local_top[:, None]), axis=1)
    row_top, exp_total, mass, self_term, cross_term, target = combined_all(
        (local_top, local_total, mass, self_term, cross_term, target), "vocab", combine_stats
    )
    log_total = jnp.log(exp_total)
    token_loss = (
        self_term / mass
        - jnp.log(mass)
        - cross_term / mass
        + row_top
        + log_total
        + hard_weight * (row_top + log_total - target)
    )
    student_probs = jnp.exp(logits - row_top[:, None]) / exp_total[:, None]
    grad = loss_scale * (
        (1.0 + hard_weight) * student_probs
        - mapped / mass[:, None]
        - hard_weight * is_target.astype(jnp.float32)
    )
    grad = grad.astype(jnp.bfloat16)
    grad_all = lax.all_gather(grad, "tok", axis=0, tiled=True)
    rows = grad_all
    hidden_grad = lax.psum_scatter(
        lax.dot_general(rows, head, (((1,), (1,)), ((), ())), preferred_element_type=jnp.float32),
        "vocab",
        scatter_dimension=0,
        tiled=True,
    )
    return (token_loss, hidden_grad)


def solution(mesh):
    in_specs = (
        P("tok", None),
        P("tok", "vocab"),
        P("tok", "vocab"),
        P("vocab", None, None),
        P(),
        P("tok"),
    )
    out_specs = (P("tok"), P("vocab", "tok"))
    return jax.shard_map(
        on_device, mesh=mesh, in_specs=in_specs, out_specs=out_specs, check_vma=False
    )
```

profile of v0, /device:TPU:0, one launch (start us, length us, event | category | flops | bytes accessed | tf_op | source)
XLA Modules:
  0.0 316.8 jit_solution(1688518700564074467)
XLA Ops:
  7.2 0.0 copy-start
  7.2 0.0 reduce-scatter.3.cloned.1.call-start
  7.2 4.2 %copy.37 = bf16[128,8192]{0,1:T(8,128)(2,1)} copy(bf16[128,8192]{1,0:T(8,128)(2,1)} %param.6) | data formatting | bytes 4194304 | tf_op args[0]
  11.4 31.1 %all_to_all.29 = bf16[128,4,2048]{0,2,1:T(8,128)(2,1)} all-to-all(bf16[128,4,2048]{0,2,1:T(8,128)(2,1)} %bitcast.89), channel_id=1, replica_groups=mesh['vocab'=32,'tok'=4] {'tok'}, dimensions={1} | all-to-all | bytes 4194304 | tf_op jit(solution)/shard_map/all_to_all | solution.py:69
  42.6 4.0 %copy.38 = bf16[4,128,2048]{2,1,0:T(8,128)(2,1)} copy(bf16[4,128,2048]{1,2,0:T(8,128)(2,1)} %bitcast.88) | data formatting | bytes 4194304 | tf_op jit(solution)/shard_map/all_to_all | solution.py:69
  46.5 14.9 %fusion.36 = f32[512,3968]{1,0:T(8,128)} fusion(bf16[512,2048]{1,0:T(8,128)(2,1)} %bitcast.92, bf16[2048,3968]{1,0:T(8,128)(2,1)} %param.7), kind=kOutput, calls=%fused_computation.71 | convolution fusion | flops 8321499136 | bytes 26476544 | tf_op jit(solution)/shard_map/dot_general | solution.py:72
  61.5 0.0 copy-start.3
  61.5 0.0 reduce-scatter.3.cloned.1.call-update
  61.5 1.3 copy-done.3
  62.7 0.0 copy-start.4
  62.7 1.5 copy.39
  64.3 2.1 copy.40
  66.4 0.0 copy-done.4
  66.4 0.1 reshape.159
  66.6 0.8 select_reduce_fusion
  67.5 0.6 convolution_convert_fusion.2
  68.1 0.0 copy-done
  68.1 0.6 convolution_convert_fusion.1
  68.7 1.7 convolution_convert_fusion
  70.4 4.6 %copy.43 = bf16[128,128,128]{2,1,0:T(8,128)(2,1)} copy(bf16[128,128,128]{2,0,1:T(8,128)(2,1)S(1)} %convolution_convert_fusion) | data formatting | bytes 8388608 | tf_op jit(solution)/shard_map/convert_element_type | solution.py:100
  75.0 8.3 %all-to-all-start.1 = ((bf16[128,128,128]{2,1,0:T(8,128)(2,1)}), bf16[128,128,128]{2,1,0:T(8,128)(2,1)}, u32[]{:S(2)}, u32[]{:S(2)}) async-start(bf16[128,128,128]{2,1,0:T(8,128)(2,1)} %copy.43), calls=%async_computation.2 | async-start | bytes 8388608 | tf_op jit(solution)/shard_map/all_to_all | solution.py:101
  83.3 0.2 all-gather.2.cloned.1.call-start
  83.6 0.1 and.29
  83.7 0.1 sub.91
  83.7 0.1 broadcast_add_fusion
  83.8 0.1 add.138
  83.9 0.1 div.44
  84.0 53.3 %all-to-all-done.1 = bf16[128,128,128]{2,1,0:T(8,128)(2,1)} async-done(((bf16[128,128,128]{2,1,0:T(8,128)(2,1)}), bf16[128,128,128]{2,1,0:T(8,128)(2,1)}, u32[]{:S(2)}, u32[]{:S(2)}) %all-to-all-start.1) | async-done | bytes 4194336 | tf_op jit(solution)/shard_map/all_to_all | solution.py:101
  137.3 5.9 %fusion.35 = (f32[128]{0:T(128)S(1)}, f32[31,128,128]{2,0,1:T(8,128)S(1)}) fusion(bf16[128,128,128]{2,1,0:T(8,128)(2,1)} %all-to-all-done.1, s32[1536]{0:T(1024)S(1)} %sub.91, s32[1536]{0:T(1024)S(1)} %fusion.25), kind=kOutput, calls=%fused_computation.70 | convolution fusion | flops 142969088 | bytes 6238720 | tf_op jit(solution)/shard_map/rkc,rj->kjc/dot_general | solution.py:110
  143.2 1.8 copy.45
  145.0 2.9 copy.46
  147.9 0.0 copy-start.5
  147.9 1.0 fusion.4
  149.0 0.0 reduce-scatter.3.cloned.1.call-done
  149.0 0.0 copy-start.2
  149.0 1.9 reduce_max.9
  150.9 0.0 copy-done.5
  150.9 0.3 copy-done.2
  151.1 2.3 fusion.5
  153.5 10.7 %all_to_all.30 = f32[32,6,128]{2,1,0:T(8,128)S(1)} all-to-all(f32[32,6,128]{2,1,0:T(8,128)S(1)} %broadcast_in_dim.21), channel_id=1, replica_groups=mesh['vocab'=32,'tok'=4] {'vocab'}, dimensions={0} | all-to-all | bytes 196608 | tf_op jit(solution)/shard_map/all_to_all | solution.py:16
  164.3 0.1 fusion.34
  165.4 0.5 fusion.29
  165.9 3.4 %fusion.8 = bf16[128,3968]{1,0:T(8,128)(2,1)} fusion(f32[128,3968]{1,0:T(8,128)} %copy.46, f32[128,3968]{1,0:T(8,128)S(1)} %copy-done.2, f32[128]{0:T(128)S(1)} %get-tuple-element.6, f32[128]{0:T(128)S(1)} %get-tuple-element.7, f32[128]{0:T(128)S(1)} %get-tuple-element.8, s32[3968]{0:T(1024)S(1)} %iota_add_fusion, s32[128]{0:T(128)S(1)} %copy-done.5), kind=kLoop, calls=%fused_computation.13 | loop fusion | flops 5079040 | bytes 5096960 | tf_op jit(solution)/shard_map/convert_element_type | solution.py:141
  169.3 0.0 all-gather.2.cloned.1.call-update
  169.3 0.0 reduce-scatter.5.cloned.1.call-start
  169.4 43.1 %all-gather.2.cloned.1.call-done = bf16[512,3968]{1,0:T(8,128)(2,1)} async-done(((bf16[128,3968]{1,0:T(8,128)(2,1)}), bf16[512,3968]{1,0:T(8,128)(2,1)}) %all-gather.2.cloned.1.call-update) | async-done | bytes 4063248 | tf_op jit(solution)/shard_map/all_gather | solution.py:142
  212.5 14.9 %fusion.37 = f32[512,2048]{1,0:T(8,128)} fusion(bf16[512,3968]{1,0:T(8,128)(2,1)} %all-gather.2.cloned.1.call-done, bf16[2048,3968]{1,0:T(8,128)(2,1)} %param.7), kind=kOutput, calls=%fused_computation.72 | convolution fusion | flops 8321499136 | bytes 24510464 | tf_op jit(solution)/shard_map/dot_general | solution.py:145
  227.3 0.0 copy-start.1
  227.3 0.0 reduce-scatter.5.cloned.1.call-update
  227.4 82.9 %reduce-scatter.5.cloned.1.call-done = f32[16,2048]{1,0:T(8,128)} async-done(((f32[512,2048]{1,0:T(8,128)}), f32[16,2048]{1,0:T(8,128)}) %reduce-scatter.5.cloned.1.call-update) | async-done | bytes 131088 | tf_op jit(solution)/shard_map/reduce_scatter | solution.py:144
  310.3 0.0 copy-done.1
  (79 shorter events, 1.0 us)
Async XLA Ops:
  7.2 60.9 %copy-start = (bf16[48,128,128]{2,1,0:T(8,128)(2,1)S(1)}, bf16[48,128,128]{2,1,0:T(8,128)(2,1)}, u32[]{:S(2)}) copy-start(bf16[48,128,128]{2,1,0:T(8,128)(2,1)} %param.9) | copy-start | bytes 4718596
  7.2 141.8 %reduce-scatter.3.cloned.1.call-start = ((), (), s32[]{:S(2)}) async-start(), calls=%async_computation.5 | async-start | bytes 10158080 | tf_op jit(solution)/shard_map/reduce_scatter | solution.py:71
  61.5 1.3 copy-start.3
  62.7 3.7 %copy-start.4 = (s32[1536,2]{0,1:T(2,128)S(1)}, s32[1536,2]{0,1:T(2,128)}, u32[]{:S(2)}) copy-start(s32[1536,2]{0,1:T(2,128)} %param.10) | copy-start | bytes 36868
  75.0 62.3 %all-to-all-start.1 = ((bf16[128,128,128]{2,1,0:T(8,128)(2,1)}), bf16[128,128,128]{2,1,0:T(8,128)(2,1)}, u32[]{:S(2)}, u32[]{:S(2)}) async-start(bf16[128,128,128]{2,1,0:T(8,128)(2,1)} %copy.43), calls=%async_computation.2 | async-start | bytes 8388608 | tf_op jit(solution)/shard_map/all_to_all | solution.py:101
  83.3 129.1 %all-gather.2.cloned.1.call-start = ((), (), s32[]{:S(2)}) async-start(), calls=%async_computation.6 | async-start | bytes 5079040 | tf_op jit(solution)/shard_map/all_gather | solution.py:142
  147.9 3.0 copy-start.5
  149.0 2.2 copy-start.2
  169.3 140.9 %reduce-scatter.5.cloned.1.call-start = ((), (), s32[]{:S(2)}) async-start(), calls=%async_computation.7 | async-start | bytes 4325376 | tf_op jit(solution)/shard_map/reduce_scatter | solution.py:144
  227.3 83.0 %copy-start.1 = (bf16[48,128,128]{2,1,0:T(8,128)(2,1)S(1)}, bf16[48,128,128]{2,1,0:T(8,128)(2,1)}, u32[]{:S(2)}) copy-start(bf16[48,128,128]{2,1,0:T(8,128)(2,1)} %param.9) | copy-start | bytes 4718596
Sparse Core Ops, SparseCore 0:
  61.6 78.7 reduce-scatter.2
  169.5 42.9 all-gather.1
  227.5 82.7 reduce-scatter.4
where the time goes:
time: 317 us
  waiting for transfers between devices  179 us (56%)
  blocking collectives  41.9 us (13%)
  matrix products  38.5 us (12%)
  local copies, waits for them, and re-layouts  24 us (8%)
  between operations  14 us (4%)
  other arithmetic  10.4 us (3%)
  starting transfers between devices  8.61 us (3%)
    reduce_scatter x1, waiting for transfers between devices, on_device(): lax.psum_scatter(lax.dot_general(rows, head, (((1,), (1,)), ((), ())), pr...  82.9 us
    all_to_all x1, waiting for transfers between devices, on_device(): lax.all_to_all(outgoing, 'vocab', split_axis=0, concat_axis=0, tiled=True)  53.3 us
    all_gather x1, waiting for transfers between devices, on_device(): grad_all = lax.all_gather(grad, 'tok', axis=0, tiled=True)  43.1 us
    all_to_all x1, blocking collectives, on_device(): lax.all_to_all(hidden, 'tok', split_axis=1, concat_axis=0, tiled=True)  31.1 us
    dot_general x1, matrix products, on_device(): jnp.dot(rows, head, preferred_element_type=jnp.float32)  14.9 us
    dot_general x1, matrix products, on_device(): lax.dot_general(rows, head, (((1,), (1,)), ((), ())), preferred_element_t...  14.9 us
    all_to_all x1, blocking collectives, sent_to_all(): lax.all_to_all(jnp.broadcast_to(shard[None], (count, *shard.shape)), axis...  10.7 us
    all_to_all x1, starting transfers between devices, on_device(): lax.all_to_all(outgoing, 'vocab', split_axis=0, concat_axis=0, tiled=True)  8.31 us
  transfers between devices with their start and end apart: 4, of which 3 were waited for; matrix products, arithmetic and copies ran while one was open for 8% of the time, Pallas kernels for 0%

commit v1 on v0

v1 whole, which is shorter than its diff:
```python
import jax
import jax.numpy as jnp
from jax import lax
from jax.experimental import pallas as pl
from jax.experimental.pallas import tpu as pltpu
from jax.sharding import PartitionSpec as P

TILE = 128
CAP = 4
NV = 32
NY = 4
QMAX = 32000.0
hard_weight = 0.5
loss_scale = 64.0
MESH = pl.DeviceIdType.MESH
CHUNKS = ((0, 1024), (1024, 1024), (2048, 1024), (3072, 896))


def dev_id(v, y):
    return (v, y)


def rcopy(src, dst, ss, rs, dev):
    return pltpu.make_async_remote_copy(
        src_ref=src, dst_ref=dst, send_sem=ss, recv_sem=rs, device_id=dev, device_id_type=MESH
    )


def where_am_i():
    v = lax.axis_index("vocab")
    y = lax.axis_index("tok")
    z, x, c = v // 8, lax.rem(v // 2, 4), lax.rem(v, 2)
    return v, y, z, x, c


def vocab_of(z, x, c):
    return (lax.rem(z, 4) * 4 + lax.rem(x, 4)) * 2 + lax.rem(c, 2)


def routing(pairs, v, blocks, row_blocks):
    nt = pairs.shape[1] // NV

    def by_source(line):
        return jnp.concatenate([line[:, i * nt : (i + 1) * nt] for i in range(NV)], axis=0)

    row, col = by_source(pairs[0:1]), by_source(pairs[1:2])
    owner = jnp.floor((col.astype(jnp.float32) + 0.5) * (1.0 / blocks)).astype(jnp.int32)
    pos = lax.broadcasted_iota(jnp.int32, owner.shape, 1)
    earlier = jnp.zeros_like(owner)
    for a in range(nt):
        hit = (owner[:, a : a + 1] == owner) & (pos > a)
        earlier = earlier + jnp.where(hit, 1, 0)
    lane = lax.broadcasted_iota(jnp.int32, (128, 128), 1)
    sub = lax.broadcasted_iota(jnp.int32, (128, 128), 0)
    src_row = lax.broadcasted_iota(jnp.int32, owner.shape, 0)
    key_row = jnp.sum(jnp.where(src_row == v, owner * CAP + earlier, 0), axis=0, keepdims=True)
    key_row = jnp.concatenate([key_row, jnp.full((1, 128 - nt), -1, jnp.int32)], axis=1)
    key_col = jnp.broadcast_to(key_row.astype(jnp.float32), (128, 128)).T
    hits = key_col == lane.astype(jnp.float32)
    slot_tile = jnp.sum(jnp.where(hits, sub, 0), axis=0, keepdims=True)
    slot_used = jnp.sum(jnp.where(hits, 1, 0), axis=0, keepdims=True)
    mine = owner == v
    pieces = []
    for k in range(CAP):
        one = mine & (earlier == k)
        got = jnp.sum(jnp.where(one, col - v * blocks - blocks, 0), axis=1, keepdims=True)
        pieces.append(got + blocks)
    col_all = jnp.broadcast_to(jnp.concatenate(pieces, axis=0).astype(jnp.float32), (128, 128))
    lane_f = lane.astype(jnp.float32)

    def summing_order(col_c, first, count_of):
        col_r = col_c.T
        before = (col_r < col_c) | ((col_r == col_c) & (lane < sub))
        rank_c = jnp.sum(jnp.where(before, 1.0, 0.0), axis=1, keepdims=True)
        at = rank_c == lane_f
        order = jnp.sum(jnp.where(at, sub, 0), axis=0, keepdims=True) - first
        same_before = (col_r == col_c) & (lane < sub)
        keep_c = jnp.max(jnp.where(same_before, 1.0, 0.0), axis=1, keepdims=True)
        keep = jnp.sum(jnp.where(at, keep_c, 0.0), axis=0, keepdims=True).astype(jnp.int32)
        upto = jnp.sum(jnp.where(col_c <= lane_f, 1, 0), axis=0, keepdims=True)
        count = jnp.sum(jnp.where(col_c == lane_f, 1, 0), axis=0, keepdims=True)
        return [
            jnp.clip(order, 0, count_of - 1),
            keep,
            jnp.clip(upto - 1, 0, count_of - 1),
            jnp.where(count > 0, 1, 0),
        ]

    early = (CAP - 1) * NV
    set_a = summing_order(jnp.where(sub < early, col_all, float(blocks)), 0, early)
    set_b = summing_order(jnp.where(sub < early, float(blocks), col_all), early, NV)
    rows = jnp.sum(jnp.where(src_row == v, row, 0), axis=0, keepdims=True)
    rows = jnp.concatenate([rows, jnp.zeros((1, 128 - nt), jnp.int32)], axis=1)
    rows_c = jnp.broadcast_to(rows.astype(jnp.float32), (128, 128)).T
    slot_row = jnp.sum(jnp.where(hits, rows_c, 0.0), axis=0, keepdims=True).astype(jnp.int32)
    slot_tile = jnp.clip(slot_tile, 0, nt - 1)
    slot_row = jnp.clip(slot_row, 0, row_blocks - 1)
    return jnp.concatenate(
        [slot_tile, slot_used, slot_row, *set_a, *set_b, jnp.zeros((5, 128), jnp.int32)], axis=0
    )


def step_kernel(
    pairs, hidden, head_hbm, teacher_hbm, tiles_hbm, ids,
    loss, out,
    logits, mapped, hid, head, teacher, tiles, feat, c_out, c_in, c_last, s_buf, part, b_out, b_in,
    tab_v, tab, stat, s_out, s_in, tids, st, st_in, gall, pp, rd, zb, xb,
    ld_sem, tab_sem, t_sem, a_ss, a_rs, f_ss, f_rs, b_ss, b_rs, s_ss, s_rs, c_ss, c_rs,
    st_ss, st_rs, e_ss, e_rs, d_ss, d_rs, z_ss, z_rs, x_ss, x_rs,
):
    v, y, z, x, c = where_am_i()
    yp, ym, y2 = lax.rem(y + 1, 4), lax.rem(y + 3, 4), lax.rem(y + 2, 4)
    partner = v + 1 - 2 * c
    nh = 8
    rows_h = head.shape[0] // nh

    loads = [
        pltpu.make_async_copy(hidden, hid, ld_sem.at[0]),
        pltpu.make_async_copy(tiles_hbm, tiles, ld_sem.at[1]),
    ] + [
        pltpu.make_async_copy(
            head_hbm.at[pl.ds(i * rows_h, rows_h)], head.at[pl.ds(i * rows_h, rows_h)], ld_sem.at[2 + i]
        )
        for i in range(nh)
    ]
    def t_copy(b):
        cols = pl.ds(pl.multiple_of(b * TILE, TILE), TILE)
        return pltpu.make_async_copy(teacher_hbm.at[:, cols], teacher.at[b], t_sem.at[b])

    loads[0].start()

    @pl.loop(0, teacher.shape[0])
    def _(b):
        t_copy(b).start()

    for ld in loads[1:]:
        ld.start()

    barrier = pltpu.get_barrier_semaphore()

    def dest_of(n):
        dc, dz, dx = n // 16, lax.rem(n // 4, 4), lax.rem(n, 4)
        return vocab_of(z + dz, x + dx, c + dc)

    def src_of(n):
        dc, dz, dx = n // 16, lax.rem(n // 4, 4), lax.rem(n, 4)
        return vocab_of(z + 4 - dz, x + 4 - dx, c + 2 - dc)

    @pl.loop(1, NV)
    def _(n):
        pl.semaphore_signal(barrier, inc=1, device_id=dev_id(dest_of(n), y), device_id_type=MESH)

    for yy in (yp, ym, y2):
        pl.semaphore_signal(barrier, inc=1, device_id=dev_id(v, yy), device_id_type=MESH)

    tab_v[...] = routing(pairs[...], v, head.shape[1] // TILE, teacher.shape[0])
    tab_copy = pltpu.make_async_copy(tab_v, tab, tab_sem.at[0])
    tab_copy.start()
    pl.semaphore_wait(barrier, NV - 1 + 3)

    kf = feat.shape[2]
    loads[0].wait()

    def a_copy(i, row, n, step, target):
        cols = pl.ds(pl.multiple_of(target * kf, kf), kf)
        row = pl.multiple_of(row, 32)
        return rcopy(
            hid.at[pl.ds(row, n), cols], feat.at[step, pl.ds(row, n)], a_ss.at[i], a_rs.at[i],
            dev_id(v, target),
        )

    a_sends = [
        a_copy(0, c * 32, 32, 0, yp),
        a_copy(1, 64 + c * 32, 32, 0, ym),
        a_copy(2, c * 64, 64, 1, y2),
        a_copy(3, 64 + c * 32, 32, 2, yp),
        a_copy(4, c * 32, 32, 2, ym),
    ]
    for cp in a_sends:
        cp.start()

    spans = ((0, 32), (64, 32), (0, 64), (64, 32), (0, 32))
    steps_of = (0, 0, 1, 2, 2)

    def forward(i, cc):
        base, n = spans[i]
        rows = pl.ds(pl.multiple_of(base + cc * n, 32), n)
        ref = feat.at[steps_of[i], rows]
        return rcopy(ref, ref, f_ss.at[i], f_rs.at[i], dev_id(partner, y))

    tab_copy.wait()
    loads[1].wait()

    @pl.loop(0, teacher.shape[0])
    def _(b):
        t_copy(b).wait()

    def slot_value(s):
        used = tab[1, s].astype(jnp.float32)
        value = jnp.dot(teacher[tab[2, s]], tiles[tab[0, s]], preferred_element_type=jnp.float32)
        return (value * used).astype(jnp.bfloat16)

    def c_slot(k, source):
        return c_last.at[source] if k == CAP - 1 else c_in.at[k * NV + source]

    def c_copy(k, n):
        return rcopy(
            c_out.at[k * NV + n], c_slot(k, v), c_ss.at[k, n], c_rs.at[k, n], dev_id(dest_of(n), y),
        )

    def send_products(k):
        @pl.loop(0, NV // 4)
        def _(g):
            values = [slot_value(dest_of(g * 4 + u) * CAP + k) for u in range(4)]
            for u in range(4):
                if u:
                    c_out[k * NV + g * 4 + u] = values[u]
                    c_copy(k, g * 4 + u).start()
                else:
                    @pl.when(g == 0)
                    def _():
                        c_slot(k, v)[...] = values[0]

                    @pl.when(g > 0)
                    def _():
                        c_out[k * NV + g * 4] = values[0]
                        c_copy(k, g * 4).start()

    send_products(0)
    send_products(1)

    def b_copy(step, q, up):
        n = CHUNKS[q][1]
        side = 0 if up else 1
        return rcopy(
            b_out.at[side, step, q, :, pl.ds(0, n)], b_in.at[side, step, q, :, pl.ds(0, n)],
            b_ss.at[side, step, q], b_rs.at[side, step, q], dev_id(v, yp if up else ym),
        )

    def s_copy(step, q, up):
        side = 0 if up else 1
        return rcopy(
            s_out.at[step, q], s_in.at[side, step, q],
            s_ss.at[side, step, q], s_rs.at[side, step, q], dev_id(v, yp if up else ym),
        )

    lane_half = lax.broadcasted_iota(jnp.int32, (1, TILE), 1) < 64
    lane64 = lax.broadcasted_iota(jnp.int32, (64, TILE), 1)
    first_col = v * logits.shape[1]
    tids[...] = jnp.broadcast_to(ids[...].astype(jnp.float32), (TILE, TILE)).T.astype(jnp.int32)

    def chunk_stats(rows, c0, width, top):
        tid = tids[rows, :] - first_col - lane64
        total, target = jnp.zeros((64, TILE), jnp.float32), jnp.zeros((64, TILE), jnp.float32)
        for t in range(c0 // TILE, (c0 + width) // TILE):
            lg = logits[rows, t * TILE : (t + 1) * TILE]
            total = total + jnp.exp(lg - top)
            target = target + jnp.where(tid == t * TILE, lg, 0.0)
        mat = jnp.where(lane64 == 0, top, 0.0)
        for i, a in ((1, total), (5, target)):
            mat = jnp.where(lane64 == i, jnp.sum(a, axis=1, keepdims=True), mat)
        return mat

    own_cols = pl.ds(pl.multiple_of(y * kf, kf), kf)
    arrivals = ((0, 1), (2,), (3, 4), ())
    forwards = []
    for step in range(4):
        for i in arrivals[step]:
            a_sends[i].wait_recv()
            fw = forward(i, c)
            fw.start()
            forwards.append(fw)
        if 1 <= step <= 2:
            send_products(step + 1)
        if step == 0:
            for ld in loads[2:]:
                ld.wait()
        for i in arrivals[step]:
            forward(i, 1 - c).wait_recv()
        for q, (c0, width) in enumerate(CHUNKS):
            def lhs():
                return feat[step] if step < 3 else hid[:, own_cols]

            n_full = width // 256

            @pl.loop(0, n_full)
            def _(t):
                cols = pl.ds(pl.multiple_of(c0 + t * 256, 256), 256)
                part[:, pl.ds(pl.multiple_of(t * 256, 256), 256)] = jnp.dot(
                    lhs(), head[:, cols], preferred_element_type=jnp.float32
                )

            if width % 256:
                part[:, n_full * 256 : width] = jnp.dot(
                    lhs(), head[:, c0 + n_full * 256 : c0 + width], preferred_element_type=jnp.float32
                )
            if step > 0:
                for up in (True, False):
                    s_copy(step - 1, q, up).wait_recv()
                line = jnp.where(lane_half, s_in[0, step - 1, q, 0:1], s_in[1, step - 1, q, 0:1])
                scales = jnp.broadcast_to(line, (TILE, TILE)).T * (1.0 / QMAX)
                for up in (True, False):
                    b_copy(step - 1, q, up).wait_recv()
            tops = []
            for side in (0, 1):
                rows = slice(side * 64, side * 64 + 64)
                top = jnp.zeros((64, 128), jnp.float32)
                for t in range(width // 128):
                    cols = slice(t * 128, (t + 1) * 128)
                    val = part[rows, cols]
                    if step > 0:
                        val = val + b_in[side, step - 1, q, :, cols].astype(jnp.float32) * scales[rows]
                    if step < 3:
                        part[rows, cols] = val
                        top = jnp.maximum(top, jnp.abs(val))
                    else:
                        logits[rows, c0 + t * 128 : c0 + (t + 1) * 128] = val
                        top = jnp.maximum(top, val) if t else val
                if step == 3:
                    stat[q, rows] = chunk_stats(rows, c0, width, jnp.max(top, axis=1, keepdims=True))
                tops.append(jnp.maximum(jnp.max(top, axis=1, keepdims=True), 1e-30))
            if step < 3:
                top = jnp.broadcast_to(jnp.concatenate(tops, axis=0), (TILE, TILE))
                s_out[step, q] = top.T[0:8]
                inv = QMAX / top
                for side in (0, 1):
                    rows = slice(side * 64, side * 64 + 64)
                    for t in range(width // 128):
                        val = part[rows, t * 128 : (t + 1) * 128] * inv[rows]
                        b_out[side, step, q, :, t * 128 : (t + 1) * 128] = (
                            jnp.round(val).astype(jnp.int32).astype(jnp.int16)
                        )
                    s_copy(step, q, side == 0).start()
                    b_copy(step, q, side == 0).start()

    lane = lax.broadcasted_iota(jnp.int32, (32, TILE), 1)
    width = logits.shape[1]
    feats = head.shape[0]
    base = v * width
    nt = width // TILE

    def c_wait(k):
        @pl.loop(1, NV)
        def _(n):
            rcopy(
                c_out.at[k * NV + n], c_slot(k, src_of(n)), c_ss.at[k, n], c_rs.at[k, n],
                dev_id(dest_of(n), y),
            ).wait_recv()

    def sum_slots(source, count, at, rows):
        def add(p, total):
            total = total * tab[at + 1, p].astype(jnp.float32)
            total = total + source[tab[at, p]][rows].astype(jnp.float32)
            s_buf[p] = total
            return total

        lax.fori_loop(0, count, add, jnp.zeros((64, TILE), jnp.float32), unroll=8)

    for k in range(CAP - 1):
        c_wait(k)
    for h in range(2):
        rows = slice(h * 64, h * 64 + 64)
        sum_slots(c_in, (CAP - 1) * NV, 3, rows)
        for j in range(nt):
            mapped[rows, j * TILE : (j + 1) * TILE] = s_buf[tab[5, j]] * tab[6, j].astype(jnp.float32)
    c_wait(CAP - 1)
    for h in range(2):
        rows = slice(h * 64, h * 64 + 64)
        sum_slots(c_last, NV, 7, rows)
        zero = jnp.zeros((64, TILE), jnp.float32)
        mass, self_t, cross = zero, zero, zero
        for j in range(nt):
            cols = slice(j * TILE, (j + 1) * TILE)
            mp = mapped[rows, cols] + s_buf[tab[9, j]] * tab[10, j].astype(jnp.float32)
            mapped[rows, cols] = mp
            mass = mass + mp
            pos = mp > 0
            self_t = self_t + jnp.where(pos, mp * jnp.log(jnp.where(pos, mp, 1.0)), 0.0)
            cross = cross + mp * logits[rows, cols]
        quarters = [stat[q, rows] for q in range(len(CHUNKS))]
        tops = [a[:, 0:1] for a in quarters]
        top = jnp.maximum(jnp.maximum(tops[0], tops[1]), jnp.maximum(tops[2], tops[3]))
        mat = jnp.zeros((64, TILE), jnp.float32)
        for a, one in zip(quarters, tops):
            mat = mat + a * jnp.where(lane64 == 1, jnp.exp(one - top), 1.0)
        mat = jnp.where(lane64 == 0, top, mat)
        for i, a in ((2, mass), (3, self_t), (4, cross)):
            mat = jnp.where(lane64 == i, jnp.sum(a, axis=1, keepdims=True), mat)
        part[rows, 0:TILE] = mat
    st[...] = part[:, 0:TILE].T[0:8]
    st_in[v] = st[...]

    @pl.loop(1, NV)
    def _(n):
        rcopy(st, st_in.at[v], st_ss.at[n], st_rs.at[n], dev_id(dest_of(n), y)).start()

    @pl.loop(1, NV)
    def _(n):
        rcopy(st, st_in.at[src_of(n)], st_ss.at[n], st_rs.at[n], dev_id(dest_of(n), y)).wait_recv()

    big = st_in[0]
    for i in range(1, NV):
        big = jnp.maximum(big, st_in[i])
    row_top = big[0:1]
    acc = jnp.zeros((8, TILE), jnp.float32)
    sub8 = lax.broadcasted_iota(jnp.int32, (8, TILE), 0)
    for i in range(NV):
        one = st_in[i]
        acc = acc + one * jnp.where(sub8 == 1, jnp.exp(one[0:1] - row_top), 1.0)
    exp_total, mass, self_term, cross_term, target = (acc[i : i + 1] for i in range(1, 6))
    log_total = jnp.log(exp_total)
    loss[...] = (
        self_term / mass - jnp.log(mass) - cross_term / mass + row_top + log_total
        + hard_weight * (row_top + log_total - target)
    )
    split = 2048
    coef = jnp.concatenate(
        [row_top, (loss_scale * (1.0 + hard_weight)) / exp_total, loss_scale / mass,
         jnp.zeros((TILE - 3, TILE), jnp.float32)], axis=0
    ).T
    part[:, 0:TILE] = coef

    def e_ref(s, kind, owner):
        first, n = ((0, 32), (0, 32), (0, 16), (16, 16))[kind]
        rows = pl.ds(pl.multiple_of(owner * 32 + first, 16), n)
        if s < 3:
            return gall.at[s, rows]
        cols = slice(0, split) if s == 3 else slice(split, width)
        return gall.at[3, rows, cols]

    def e_copy(s, kind):
        ref = e_ref(s, kind, (y, y, ym, yp)[kind])
        return rcopy(ref, ref, e_ss.at[s, kind], e_rs.at[s, kind], dev_id(v, yp if kind % 2 == 0 else ym))

    def e_wait(s, kind):
        ref = e_ref(s, kind, (ym, yp, y2, y2)[kind])
        rcopy(ref, ref, e_ss.at[s, kind], e_rs.at[s, kind], dev_id(v, yp if kind % 2 == 0 else ym)).wait_recv()

    def grad_rows(s):
        j = lax.rem(s + y, 4)
        r0 = pl.multiple_of(j * 32, 32)
        rows = pl.ds(r0, 32)
        tid = tids[rows, :] - base - lane
        cf = part[rows, 0:TILE]
        top = jnp.broadcast_to(cf[:, 0:1], (32, TILE))
        ce = jnp.broadcast_to(cf[:, 1:2], (32, TILE))
        cm = jnp.broadcast_to(cf[:, 2:3], (32, TILE))
        g0 = pl.multiple_of(y * 32, 32)
        for t in range(nt):
            cols = slice(t * TILE, (t + 1) * TILE)
            val = ce * jnp.exp(logits[rows, cols] - top) - cm * mapped[rows, cols]
            val = val - jnp.where(tid == t * TILE, loss_scale * hard_weight, 0.0)
            gall[s, pl.ds(g0, 32), cols] = val.astype(jnp.bfloat16)

    def own_out(s):
        e_copy(s, 0).start()
        e_copy(s, 1).start()

    for s in range(4):
        grad_rows(s)
        if s < 2:
            own_out(s)


    hf = feats // 2

    def d_copy(s, h):
        return rcopy(pp.at[s, h, 1 - c], rd.at[s, h], d_ss.at[s, h], d_rs.at[s, h], dev_id(partner, y))

    def one_copy(s, h, d):
        if h == 0:
            zt = lax.rem(z + d, 4)
            slot, to = zt, vocab_of(zt, x, c)
        else:
            xt = lax.rem(x + d, 4)
            slot, to = lax.rem(xt + 4 - s, 4), vocab_of(z, xt, c)
        return rcopy(pp.at[s, h, c, slot], zb.at[s, h, d - 1], z_ss.at[s, h, d - 1], z_rs.at[s, h, d - 1], dev_id(to, y))

    def one_phase(s, h):
        d_copy(s, h).wait_recv()
        for i in range(4):
            pp[s, h, c, i] = pp[s, h, c, i] + rd[s, h, i]
        for d in (2, 1, 3):
            one_copy(s, h, d).start()

    def own_slot(s, h):
        return z if h == 0 else lax.rem(x + 4 - s, 4)

    def two_dist(s, h):
        return lax.rem(s + z + 4 - x, 4) if h == 0 else lax.rem(x + 8 - s - z, 4)

    def two_copy(s, h, d):
        to = vocab_of(z, x + d, c) if h == 0 else vocab_of(z + d, x, c)
        return rcopy(pp.at[s, h, c, own_slot(s, h)], xb.at[h, d - 1], x_ss.at[s, h], x_rs.at[h, d - 1], dev_id(to, y))

    def two_phase(s, h):
        for d in (1, 2, 3):
            one_copy(s, h, d).wait_recv()
        own = own_slot(s, h)
        pp[s, h, c, own] = (pp[s, h, c, own] + zb[s, h, 0]) + (zb[s, h, 1] + zb[s, h, 2])
        for d in (1, 2, 3):
            @pl.when(two_dist(s, h) == d)
            def _():
                two_copy(s, h, d).start()

    def pass_on(s):
        e_wait(s, 0)
        e_copy(s, 2).start()
        e_wait(s, 1)
        e_copy(s, 3).start()

    def product(s, half, k0, k1, more=False):
        @pl.loop(0, hf // 512)
        def _(f):
            res = lax.dot_general(
                gall[s, :, k0:k1], head[pl.ds(pl.multiple_of(half * hf + f * 512, 512), 512), k0:k1],
                (((1,), (1,)), ((), ())), preferred_element_type=jnp.float32,
            )
            fr = pl.ds(pl.multiple_of(f * 512, 512), 512)
            for o in range(4):
                for h in range(2):
                    a = o * 32 + h * 16
                    value = res[a : a + 16]
                    if more:
                        value = value + pp[s, half, h, o, :, fr]
                    pp[s, half, h, o, :, fr] = value

    pass_on(0)
    own_out(2)
    for s in range(3):
        pass_on(s + 1)
        if s == 0:
            own_out(3)
        if s == 1:
            own_out(4)
        if s >= 1:
            one_phase(s - 1, 0)
            one_phase(s - 1, 1)
        if s >= 2:
            two_phase(s - 2, 0)
            two_phase(s - 2, 1)
        e_wait(s, 2)
        e_wait(s, 3)
        product(s, 0, 0, width)
        d_copy(s, 0).start()
        if s == 2:
            pass_on(4)
        product(s, 1, 0, width)
        d_copy(s, 1).start()
    for kind in (2, 3):
        e_wait(3, kind)
    product(3, 0, 0, split)
    one_phase(2, 0)
    one_phase(2, 1)
    two_phase(1, 0)
    two_phase(1, 1)
    product(3, 1, 0, split)
    for kind in (2, 3):
        e_wait(4, kind)
    product(3, 0, split, width, True)
    d_copy(3, 0).start()
    product(3, 1, split, width, True)
    d_copy(3, 1).start()
    one_phase(3, 0)
    one_phase(3, 1)
    two_phase(2, 0)
    two_phase(2, 1)
    two_phase(3, 0)
    two_phase(3, 1)
    own_last = (z, z)
    for h in range(2):
        for d in (1, 2, 3):
            two_copy(0, h, d).wait_recv()
        mine = pp[lax.rem(x + 4 - z, 4), h, c, own_last[h]]
        out[:, h * hf : (h + 1) * hf] = (mine + xb[h, 0]) + (xb[h, 1] + xb[h, 2])

    for s in range(5):
        for kind in range(4):
            e_copy(s, kind).wait_send()
    for s in range(4):
        for h in range(2):
            d_copy(s, h).wait_send()
            for d in (1, 2, 3):
                one_copy(s, h, d).wait_send()
            for d in (1, 2, 3):
                @pl.when(two_dist(s, h) == d)
                def _():
                    two_copy(s, h, d).wait_send()

    @pl.loop(1, NV)
    def _(n):
        rcopy(st, st_in.at[v], st_ss.at[n], st_rs.at[n], dev_id(dest_of(n), y)).wait_send()

    for cp in a_sends + forwards:
        cp.wait_send()
    for step in range(3):
        for q in range(4):
            for up in (True, False):
                b_copy(step, q, up).wait_send()
                s_copy(step, q, up).wait_send()

    for k in range(CAP):
        @pl.loop(1, NV)
        def _(n):
            c_copy(k, n).wait_send()


def any_spec():
    return pl.BlockSpec(memory_space=pl.ANY)


def vmem_spec():
    return pl.BlockSpec(memory_space=pltpu.VMEM)


def on_device(hidden, head, teacher_probs, tile_values, tile_list, token_ids):
    tok, width = hidden.shape[0], head.shape[1]
    feats, nt = head.shape[0], tile_values.shape[0]
    dma = pltpu.SemaphoreType.DMA
    f32, bf16, i16 = jnp.float32, jnp.bfloat16, jnp.int16
    loss, out = pl.pallas_call(
        step_kernel,
        out_shape=(jax.ShapeDtypeStruct((1, tok), f32), jax.ShapeDtypeStruct((16, feats), f32)),
        in_specs=[vmem_spec()] + [any_spec()] * 4 + [vmem_spec()],
        out_specs=(vmem_spec(),) * 2,
        scratch_shapes=[
            pltpu.VMEM((tok, width), f32),
            pltpu.VMEM((tok, width), f32),
            pltpu.VMEM(hidden.shape, bf16),
            pltpu.VMEM(head.shape, bf16),
            pltpu.VMEM((teacher_probs.shape[1] // TILE, tok, TILE), bf16),
            pltpu.VMEM(tile_values.shape, bf16),
            pltpu.VMEM((3, tok, feats), bf16),
            pltpu.VMEM((NV * CAP, tok, TILE), bf16),
            pltpu.VMEM((NV * (CAP - 1), tok, TILE), bf16),
            pltpu.VMEM((NV, tok, TILE), bf16),
            pltpu.VMEM((NV * (CAP - 1), 64, TILE), f32),
            pltpu.VMEM((tok, 1024), f32),
            pltpu.VMEM((2, 3, 4, 64, 1024), i16),
            pltpu.VMEM((2, 3, 4, 64, 1024), i16),
            pltpu.VMEM((16, TILE), jnp.int32),
            pltpu.SMEM((16, TILE), jnp.int32),
            pltpu.VMEM((len(CHUNKS), tok, TILE), f32),
            pltpu.VMEM((3, 4, 8, TILE), f32),
            pltpu.VMEM((2, 3, 4, 8, TILE), f32),
            pltpu.VMEM((TILE, TILE), jnp.int32),
            pltpu.VMEM((8, TILE), f32),
            pltpu.VMEM((NV, 8, TILE), f32),
            pltpu.VMEM((4, tok, width), bf16),
            pltpu.VMEM((4, 2, 2, 4, 16, feats // 2), f32),
            pltpu.VMEM((4, 2, 4, 16, feats // 2), f32),
            pltpu.VMEM((4, 2, 3, 16, feats // 2), f32),
            pltpu.VMEM((2, 3, 16, feats // 2), f32),
            dma((10,)), dma((1,)), dma((teacher_probs.shape[1] // TILE,)), dma((5,)), dma((5,)), dma((5,)), dma((5,)),
            dma((2, 3, 4)), dma((2, 3, 4)), dma((2, 3, 4)), dma((2, 3, 4)), dma((CAP, NV)), dma((CAP, NV)),
            dma((NV,)), dma((NV,)), dma((5, 4)), dma((5, 4)), dma((4, 2)), dma((4, 2)),
            dma((4, 2, 3)), dma((4, 2, 3)), dma((4, 2)), dma((2, 3)),
        ],
        compiler_params=pltpu.CompilerParams(
            collective_id=0, has_side_effects=True, vmem_limit_bytes=67043328
        ),
        name="step",
    )(tile_list.T, hidden, head, teacher_probs, tile_values, token_ids.reshape(1, tok))
    return loss.reshape(tok), out


def solution(mesh):
    in_specs = (
        P("tok", None), P("tok", "vocab"), P("tok", "vocab"), P("vocab", None, None), P(), P("tok"),
    )
    out_specs = (P("tok"), P("vocab", "tok"))
    return jax.shard_map(on_device, mesh=mesh, in_specs=in_specs, out_specs=out_specs, check_vma=False)
```

time: 317 us -> 132 us (0.42)
  waiting for transfers between devices: 179 us -> 0 us
  Pallas kernels: 0 us -> 127 us
  blocking collectives: 41.9 us -> 0 us
  matrix products: 38.5 us -> 0 us
  local copies, waits for them, and re-layouts: 24 us -> 2.74 us
  between operations: 14 us -> 0.64 us
  other arithmetic: 10.4 us -> 0 us
  starting transfers between devices: 8.61 us -> 0 us
    pallas_call x0 -> x1, Pallas kernels: none -> 127 us  [on_device(): pl.pallas_call(step_kernel, out_shape=(jax.ShapeDtypeStruct((1, tok), f32...]
    reduce_scatter x2 -> x0, waiting for transfers between devices: 82.9 us -> none  [the longest x1 82.9 us: on_device(): lax.psum_scatter(lax.dot_general(rows, head, (((1,), (1,)), ((), ())), pr...]
    all_to_all x1 -> x0, waiting for transfers between devices: 53.3 us -> none  [on_device(): lax.all_to_all(outgoing, 'vocab', split_axis=0, concat_axis=0, tiled=True)]
    all_gather x1 -> x0, waiting for transfers between devices: 43.1 us -> none  [on_device(): grad_all = lax.all_gather(grad, 'tok', axis=0, tiled=True)]
    all_to_all x2 -> x0, blocking collectives: 41.9 us -> none  [the longest x1 31.1 us: on_device(): lax.all_to_all(hidden, 'tok', split_axis=1, concat_axis=0, tiled=True)]
    dot_general x6 -> x0, matrix products: 38.5 us -> none  [the longest x1 14.9 us: on_device(): jnp.dot(rows, head, preferred_element_type=jnp.float32)]
    all_to_all x1 -> x0, starting transfers between devices: 8.31 us -> none  [on_device(): lax.all_to_all(outgoing, 'vocab', split_axis=0, concat_axis=0, tiled=True)]
    reshape x3 -> x0, local copies, waits for them, and re-layouts: 5.11 us -> none  [the longest x1 2.89 us: on_device(): mapped = mapped.reshape(tok_count, vocab_part)]
  transfers between devices with their start and end apart: 4 -> 0, of which waited for: 3 -> 0; matrix products, arithmetic and copies ran while one was open for 8% -> 0% of each run, Pallas kernels for 0% -> 0%
where the time goes in v1:
time: 132 us; the launch traced here: 130 us
  Pallas kernels  127 us (96%)
  local copies, waits for them, and re-layouts  2.74 us (2%)
    pallas_call x1, Pallas kernels, on_device(): pl.pallas_call(step_kernel, out_shape=(jax.ShapeDtypeStruct((1, tok), f32...  127 us
    unnamed x2, local copies, waits for them, and re-layouts  2.74 us

profile of v1, /device:TPU:0, one launch (start us, length us, event | category | flops | bytes accessed | tf_op | source)
XLA Modules:
  0.0 130.2 jit_solution(144265885990144911)
XLA Ops:
  0.6 126.8 %step.1 = (f32[1,128]{1,0:T(1,128)}, f32[16,2048]{1,0:T(8,128)}) custom-call(s32[2,1536]{1,0:T(2,128)} %bitcast.3, bf16[128,8192]{1,0:T(8,128)(2,1)} %hidden.1, bf16[2048,3968]{1,0:T(8,128)(2,1)} %head_hbm.1, bf16[128,4736]{1,0:T(8,128)(2,1)} %teacher_hbm.1, bf16[48,128,128]{2,1,0:T(8,128)(2,1)} %tiles_hbm.1, s32[1,128]{1,0:T(1,128)} %bitcast.4), custom_call_target="tpu_custom_call" | custom-call | tf_op jit(solution)/shard_map/step/pallas_call | solution.py:621
  127.4 1.2 copy.10
  128.6 1.6 %copy.11 = f32[16,2048]{1,0:T(8,128)} copy(f32[16,2048]{1,0:T(8,128)} %get-tuple-element.9) | data formatting | bytes 262144
